TPU v7x, 256 devices: a whole 4x4x8 slice. The times are simulated.
256 devices in a mesh: dp: 16 (over y, x_hi, core), space: 16 (over x_lo, z).
Axes of the slice: x: 4 (x_hi: 2, x_lo: 2; x = x_hi * 2 + x_lo), y: 4, z: 8, core: 2. Of those that a mesh axis runs over, the one named last changes fastest.
Arguments:
- act_in: bfloat16 [16, 32, 64, 2048], P('dp', 'space'), may hold values from -6 to 6
- weight_one: bfloat16 [3, 3, 3, 32, 64], replicated, may hold values from -0.21875 to 0.21875
- bias_one: float32 [64], replicated, may hold values from -3 to 3
- weight_two: bfloat16 [3, 3, 3, 64, 128], replicated, may hold values from -0.15625 to 0.15625
- bias_two: float32 [128], replicated, may hold values from -3 to 3
- cotangent: bfloat16 [16, 16, 32, 4096], P('dp', 'space'), may hold values from -24 to 24
Outputs:
- grad_input: bfloat16 [16, 32, 64, 2048], P('dp', 'space')
- grad_w_one: float32 [3, 3, 3, 32, 64], replicated
- grad_b_one: float32 [64], replicated
- grad_w_two: float32 [3, 3, 3, 64, 128], replicated
- grad_b_two: float32 [128], replicated
All inputs are finite; a program needn't handle non-finite values.
Results may differ from a plain program's by a relative error of at most 0.01.
Values may be sent and summed in bfloat16 or wider, within the bound.
No kernel may reach another device: no remote copies, remote signals or barrier semaphores. Data moves between devices by JAX's collectives and lax.ppermute only.
A program may use at most 128 MiB of HBM per device.

v0:
```python
import math
import jax
import jax.numpy as jnp
from jax import lax
from jax.sharding import PartitionSpec as P


def padded_2(cells, sides, width):
    for axis, dim in sides:
        count = lax.axis_size(axis)
        ends = count - 1
        head = lax.slice_in_dim(cells, 0, width, axis=dim)
        tail = lax.slice_in_dim(cells, cells.shape[dim] - width, cells.shape[dim], axis=dim)
        cells = jnp.concatenate(
            [
                lax.ppermute(tail, axis, [(i, (i + 1) % count) for i in range(ends)]),
                cells,
                lax.ppermute(head, axis, [((i + 1) % count, i) for i in range(ends)]),
            ],
            axis=dim,
        )
    return cells


def forward_conv(padded, kernel):
    return lax.conv_general_dilated(
        padded,
        kernel,
        (1, 1, 1),
        ((0, 0), (1, 1), (1, 1)),
        dimension_numbers=("NDHWC", "DHWIO", "NDHWC"),
        preferred_element_type=jnp.float32,
    )


def weight_grad(padded, delta):
    return lax.conv_general_dilated(
        padded,
        delta,
        (1, 1, 1),
        ((0, 0), (1, 1), (1, 1)),
        dimension_numbers=("CDHWN", "IDHWO", "DHWNC"),
        preferred_element_type=jnp.float32,
    )


def input_grad(delta, kernel, depth_pad):
    return lax.conv_general_dilated(
        delta,
        kernel[::-1, ::-1, ::-1],
        (1, 1, 1),
        (depth_pad, (1, 1), (1, 1)),
        dimension_numbers=("NDHWC", "DHWOI", "NDHWC"),
        preferred_element_type=jnp.float32,
    )


def silu_slope(value):
    sig = jax.nn.sigmoid(value)
    return sig * (1.0 + value * (1.0 - sig))


def local(act_in, weight_one, bias_one, weight_two, bias_two, cotangent):
    samples, slab, side, merged = act_in.shape
    chan_in = weight_one.shape[3]
    chan_mid = weight_one.shape[4]
    chan_out = weight_two.shape[4]
    half = side // 2
    slab_two = slab // 2
    batch_all = samples * lax.axis_size("dp")
    depth_all = slab * lax.axis_size("space")
    scale_one = 16.0 / math.sqrt(batch_all * depth_all * side * side)
    scale_two = 1.0 / math.sqrt(batch_all * (depth_all // 2) * half * half)
    x_pad = padded_2(act_in, (("space", 1),), 1).reshape(samples, slab + 2, side, side, chan_in)
    pre_one = forward_conv(x_pad, weight_one) + bias_one
    act_one = pre_one * jax.nn.sigmoid(pre_one)
    pooled = (
        act_one.reshape(samples, slab_two, 2, half, 2, half, 2, chan_mid)
        .mean(axis=(2, 4, 6))
        .astype(jnp.bfloat16)
    )
    pool_pad = padded_2(
        pooled.reshape(samples, slab_two, half, half * chan_mid), (("space", 1),), 1
    ).reshape(samples, slab_two + 2, half, half, chan_mid)
    pre_two = forward_conv(pool_pad, weight_two) + bias_two
    cot_five = cotangent.reshape(samples, slab_two, half, half, chan_out)
    delta_two = (cot_five.astype(jnp.float32) * silu_slope(pre_two)).astype(jnp.bfloat16)
    gw_two = weight_grad(pool_pad, delta_two)
    gb_two = jnp.sum(delta_two, axis=(0, 1, 2, 3), dtype=jnp.float32)
    gw_two, gb_two = lax.psum((gw_two, gb_two), ("dp", "space"))
    delta_pad = padded_2(
        delta_two.reshape(samples, slab_two, half, half * chan_out), (("space", 1),), 1
    ).reshape(samples, slab_two + 2, half, half, chan_out)
    grad_pooled = input_grad(delta_pad, weight_two, (0, 0))
    spread = jnp.broadcast_to(
        grad_pooled[:, :, None, :, None, :, None, :],
        (samples, slab_two, 2, half, 2, half, 2, chan_mid),
    ).reshape(samples, slab, side, side, chan_mid)
    delta_one = (spread / 8.0 * silu_slope(pre_one)).astype(jnp.bfloat16)
    gw_one = weight_grad(x_pad, delta_one)
    gb_one = jnp.sum(delta_one, axis=(0, 1, 2, 3), dtype=jnp.float32)
    delta_one_pad = padded_2(
        delta_one.reshape(samples, slab, side, side * chan_mid), (("space", 1),), 1
    ).reshape(samples, slab + 2, side, side, chan_mid)
    grad_x = input_grad(delta_one_pad, weight_one, (0, 0))
    gw_one, gb_one = lax.psum((gw_one, gb_one), ("dp", "space"))
    grad_input = grad_x.astype(jnp.bfloat16).reshape(samples, slab, side, side * chan_in)
    return (
        grad_input,
        gw_one * scale_one,
        gb_one * scale_one,
        gw_two * scale_two,
        gb_two * scale_two,
    )


def solution(mesh):
    placed = (P("dp", "space", None, None), P(), P(), P(), P(), P("dp", "space", None, None))
    return jax.shard_map(
        local,
        mesh=mesh,
        in_specs=placed,
        out_specs=(P("dp", "space", None, None), P(), P(), P(), P()),
        check_vma=False,
    )
```

profile of v0, /device:TPU:1, one launch (start us, length us, event | category | flops | bytes accessed | tf_op | source)
XLA Modules:
  0.0 471.9 jit_solution(11770701972416479829)
XLA Ops:
  7.2 1.6 copy.175
  8.9 4.4 collective-permute-start
  13.3 1.3 collective-permute-start.1
  14.6 9.3 %collective-permute-done = bf16[1,1,64,2048]{2,3,1,0:T(8,128)(2,1)S(1)} collective-permute-done((bf16[1,1,64,2048]{2,3,1,0:T(8,128)(2,1)S(1)}, bf16[1,1,64,2048]{2,3,1,0:T(8,128)(2,1)S(1)}, u32[]{:S(2)}, u32[]{:S(2)}) %collective-permute-start) | collective-permute-done | bytes 262176 | tf_op jit(solution)/shard_map/ppermute | solution.py:16
  23.8 4.2 collective-permute-done.1
  28.0 1.7 pad_maximum_fusion
  29.7 1.9 pad
  31.7 6.7 %copy.179 = bf16[4,64,1,8,9,32]{5,3,4,1,0,2:T(8,128)(2,1)} copy(bf16[4,64,1,8,9,32]{1,5,4,3,0,2:T(8,128)(2,1)} %bitcast.114) | data formatting | bytes 2359296 | tf_op jit(solution)/shard_map/conv_general_dilated | solution.py:26
  38.4 1.5 slice.27
  40.0 11.3 %fusion.16 = (f32[2,64,8,9,64]{4,2,3,1,0:T(8,128)S(1)}, f32[2,64,8,9,64]{4,2,3,1,0:T(8,128)}) fusion(f32[64]{0:T(128)S(1)} %copy-done.9, pred[8,9]{0,1:T(8,128)(4,1)S(1)} %copy-done.11, bf16[3,3,3,32,64]{4,3,2,1,0:T(8,128)(2,1)S(1)} %copy-done.7, bf16[4,64,1,7,2,32]{5,3,4,1,0,2:T(8,128)(2,1)S(1)} %slice.27, bf16[4,64,1,8,9,32]{5,3,4,1,0,2:T(8,128)(2,1)} %copy.179), kind=kOutput, calls=%fused_computation.18 | convolution fusion | flops 1018822656 | bytes 6238536 | tf_op jit(solution)/shard_map/conv_general_dilated | solution.py:26
  51.3 0.9 copy.180
  52.2 2.0 slice_reduce_fusion
  54.2 3.3 reduce_sum.36
  57.7 0.3 convert_element_type.57
  57.9 4.2 collective-permute-start.2
  62.3 1.5 collective-permute-start.3
  63.8 5.5 %copy.198 = f32[2,64,8,9,64]{4,1,3,2,0:T(8,128)} copy(f32[2,64,8,9,64]{4,2,3,1,0:T(8,128)} %get-tuple-element.42) | data formatting | bytes 4718592 | tf_op jit(solution)/shard_map/mul | solution.py:60
  69.3 13.0 %copy.205 = bf16[1,4,64,64,32]{4,0,3,2,1:T(2,128)(2,1)} copy(bf16[1,4,64,64,32]{2,4,3,1,0:T(8,128)(2,1)S(1)} %bitcast.106) | data formatting | bytes 2097152 | tf_op jit(solution)/shard_map/reshape | solution.py:74
  82.3 1.2 concatenate.41
  83.6 0.5 constant_dynamic-update-slice_fusion.1
  84.1 0.6 copy_dynamic-update-slice_fusion
  84.7 1.2 concatenate.42
  86.0 0.6 constant_dynamic-update-slice_fusion
  86.6 0.9 copy.236
  87.5 0.2 pad.2.clone
  87.7 0.4 copy.188
  88.2 1.5 add_multiply_fusion.1
  89.7 0.1 copy.189
  89.9 0.8 convert_reduce_fusion.1
  90.7 0.1 reshape.106
  90.8 4.9 %collective-permute-start.4 = (bf16[1,1,32,4096]{3,2,1,0:T(8,128)(2,1)S(1)}, bf16[1,1,32,4096]{3,2,1,0:T(8,128)(2,1)S(1)}, u32[]{:S(2)}, u32[]{:S(2)}) collective-permute-start(bf16[1,1,32,4096]{3,2,1,0:T(8,128)(2,1)S(1)} %reshape.106), channel_id=1, source_target_pairs={{0,1},{1,2},{2,3},{3,4},{4,5},{5,6},{6,7},{7,8},{8,9},{9,10},{10,1... | collective-permute-start | bytes 786440 | tf_op jit(solution)/shard_map/ppermute | solution.py:16
  95.7 1.7 collective-permute-start.5
  97.4 8.1 %fusion.56 = f32[3,3,3,64,128]{4,3,2,1,0:T(8,128)} fusion(bf16[1,3,32,32,64]{4,0,3,2,1:T(2,128)(2,1)S(1)} %constant_dynamic-update-slice_fusion, bf16[1,1,32,32,128]{4,3,1,2,0:T(8,128)(2,1)S(1)} %get-tuple-element.40), kind=kOutput, calls=%fused_computation.65 | convolution fusion | flops 434307072 | bytes 1540096 | tf_op jit(solution)/shard_map/conv_general_dilated | solution.py:37
  105.7 0.3 copy.212
  106.1 0.4 copy.196
  106.6 2.5 fusion.47
  109.1 0.1 copy.197
  109.3 1.0 broadcast_in_dim.4
  110.3 0.8 fusion.17
  111.1 1.4 copy-done.2
  112.5 1.5 copy.238
  114.0 2.5 reshape.107
  116.5 2.3 fusion.71
  118.8 5.7 %collective-permute-start.6 = (bf16[1,1,64,4096]{3,2,1,0:T(8,128)(2,1)}, bf16[1,1,64,4096]{3,2,1,0:T(8,128)(2,1)}, u32[]{:S(2)}, u32[]{:S(2)}) collective-permute-start(bf16[1,1,64,4096]{3,2,1,0:T(8,128)(2,1)} %get-tuple-element.45), channel_id=1, source_target_pairs={{0,1},{1,2},{2,3},{3,4},{4,5},{5,6},{6,7},{7,8},{8,9},{9,10},{10,1... | collective-permute-start | bytes 1572872 | tf_op jit(solution)/shard_map/ppermute | solution.py:16
  124.5 1.3 collective-permute-start.7
  125.8 66.2 %fusion.18 = f32[3,3,3,32,64]{4,3,2,1,0:T(8,128)} fusion(bf16[1,4,64,64,32]{4,0,3,2,1:T(2,128)(2,1)} %copy.205, bf16[1,2,64,64,64]{4,3,2,1,0:T(8,128)(2,1)S(1)} %bitcast.108), kind=kOutput, calls=%fused_computation.25 | convolution fusion | flops 887193600 | bytes 2318336 | tf_op jit(solution)/shard_map/conv_general_dilated | solution.py:37
  192.0 2.8 convert_reduce_fusion
  194.8 83.0 %all-reduce = (f32[64]{0:T(128)S(1)}, f32[128]{0:T(128)S(1)}) all-reduce(f32[64]{0:T(128)S(1)} %convert_reduce_fusion, f32[128]{0:T(128)S(1)} %copy-done.6), channel_id=1, replica_groups=mesh['dp'=16,'space'=16] {'dp','space'}, use_global_device_ids=true, to_apply=%region_4.0 | all-reduce | flops 192 | bytes 1536 | tf_op jit(solution)/shard_map/psum | solution.py:106
  277.9 0.5 broadcast_multiply_fusion.2
  278.4 0.5 broadcast_multiply_fusion.3
  278.9 2.8 concatenate.34
  281.7 2.8 concatenate.35
  284.4 2.2 maximum_bitcast_fusion
  286.7 2.7 copy.213
  289.4 1.3 pad.6.clone
  290.7 3.0 copy.203
  293.7 0.3 slice.36
  294.0 18.1 %fusion.4 = bf16[2,64,8,9,32]{4,2,3,1,0:T(8,128)(2,1)} fusion(bf16[3,3,3,32,64]{4,3,2,1,0:T(8,128)(2,1)S(1)} %copy-done.8, bf16[4,64,1,7,2,64]{5,3,4,1,0,2:T(8,128)(2,1)S(1)} %slice.36, bf16[4,64,1,8,9,64]{5,3,4,1,0,2:T(8,128)(2,1)S(1)} %copy.203), kind=kOutput, calls=%fused_computation.6 | convolution fusion | flops 1017249792 | bytes 3518464 | tf_op jit(solution)/shard_map/conv_general_dilated | solution.py:48
  312.1 3.2 copy.204
  315.3 0.3 select_convert_fusion
  315.7 1.1 copy.208
  316.9 143.7 %all-reduce.4.cloned.1.call-done = (f32[3,3,3,32,64]{4,3,2,1,0:T(8,128)}, f32[3,3,3,64,128]{4,3,2,1,0:T(8,128)}) async-done(((f32[3,3,3,32,64]{4,3,2,1,0:T(8,128)}, f32[3,3,3,64,128]{4,3,2,1,0:T(8,128)}), (f32[3,3,3,32,64]{4,3,2,1,0:T(8,128)}, f32[3,3,3,64,128]{4,3,2,1,0:T(8,128)})) %all-reduce.4.cloned.1.call-update) | async-done | bytes 1105936 | tf_op jit(solution)/shard_map/psum | solution.py:106
  460.6 2.2 broadcast_multiply_fusion
  462.8 1.8 broadcast_multiply_fusion.1
  (52 shorter events, 1.1 us)
Async XLA Ops:
  7.2 81.0 %copy-start = (bf16[3,3,3,64,128]{4,3,2,1,0:T(8,128)(2,1)S(1)}, bf16[3,3,3,64,128]{4,3,2,1,0:T(8,128)(2,1)}, u32[]{:S(2)}) copy-start(bf16[3,3,3,64,128]{4,3,2,1,0:T(8,128)(2,1)} %param.9) | copy-start | bytes 1327108
  7.2 453.4 %all-reduce.4.cloned.1.call-start = ((), (), s32[]{:S(2)}) async-start(), calls=%async_computation | async-start | bytes 2654208 | tf_op jit(solution)/shard_map/psum | solution.py:106
  8.8 15.0 %copy-start.3 = (bf16[1,2,64,2048]{2,3,1,0:T(8,128)(2,1)}, bf16[1,2,64,2048]{2,3,1,0:T(8,128)(2,1)S(1)}, u32[]{:S(2)}) copy-start(bf16[1,2,64,2048]{2,3,1,0:T(8,128)(2,1)S(1)} %copy.175) | copy-start | bytes 1572868
  8.9 15.0 %collective-permute-start = (bf16[1,1,64,2048]{2,3,1,0:T(8,128)(2,1)S(1)}, bf16[1,1,64,2048]{2,3,1,0:T(8,128)(2,1)S(1)}, u32[]{:S(2)}, u32[]{:S(2)}) collective-permute-start(bf16[1,1,64,2048]{2,3,1,0:T(8,128)(2,1)S(1)} %get-tuple-element.47), channel_id=1, source_target_pairs={{0,1},{1,2},{2,3},{3,4},{4,5},{5,6},{6,7},{7,8},{8,9},{9,10},{10,1... | collective-permute-start | bytes 786440 | tf_op jit(solution)/shard_map/ppermute | solution.py:16
  13.3 14.7 %collective-permute-start.1 = (bf16[1,1,64,2048]{2,3,1,0:T(8,128)(2,1)S(1)}, bf16[1,1,64,2048]{2,3,1,0:T(8,128)(2,1)S(1)}, u32[]{:S(2)}, u32[]{:S(2)}) collective-permute-start(bf16[1,1,64,2048]{2,3,1,0:T(8,128)(2,1)S(1)} %get-tuple-element.48), channel_id=1, source_target_pairs={{1,0},{2,1},{3,2},{4,3},{5,4},{6,5},{7,6},{8,7},{9,8},{10,9},{11,1... | collective-permute-start | bytes 786440 | tf_op jit(solution)/shard_map/ppermute | solution.py:18
  31.7 8.3 %copy-start.7 = (bf16[3,3,3,32,64]{4,3,2,1,0:T(8,128)(2,1)S(1)}, bf16[3,3,3,32,64]{4,3,2,1,0:T(8,128)(2,1)}, u32[]{:S(2)}) copy-start(bf16[3,3,3,32,64]{4,3,2,1,0:T(8,128)(2,1)} %param.7) | copy-start | bytes 331780
  31.7 8.3 %copy-start.9 = (f32[64]{0:T(128)S(1)}, f32[64]{0:T(128)}, u32[]{:S(2)}) copy-start(f32[64]{0:T(128)} %param.8) | copy-start | bytes 772
  31.7 8.3 %copy-start.11 = (pred[8,9]{0,1:T(8,128)(4,1)S(1)}, pred[8,9]{0,1:T(8,128)(4,1)}, u32[]{:S(2)}) copy-start(pred[8,9]{0,1:T(8,128)(4,1)} %constant.38) | copy-start | bytes 220
  52.2 10.0 %copy-start.4 = (bf16[1,1,32,4096]{3,2,1,0:T(8,128)(2,1)S(1)}, bf16[1,1,32,4096]{3,2,1,0:T(8,128)(2,1)}, u32[]{:S(2)}) copy-start(bf16[1,1,32,4096]{3,2,1,0:T(8,128)(2,1)} %param.11) | copy-start | bytes 786436
  57.9 24.4 %collective-permute-start.2 = (bf16[1,1,32,2048]{3,2,1,0:T(8,128)(2,1)S(1)}, bf16[1,1,32,2048]{3,2,1,0:T(8,128)(2,1)}, u32[]{:S(2)}, u32[]{:S(2)}) collective-permute-start(bf16[1,1,32,2048]{3,2,1,0:T(8,128)(2,1)S(1)} %convert_element_type.57), channel_id=1, source_target_pairs={{0,1},{1,2},{2,3},{3,4},{4,5},{5,6},{6,7},{7,8},{8,9},{9,10},{10,1... | collective-permute-start | bytes 393224 | tf_op jit(solution)/shard_map/ppermute | solution.py:16
  62.3 22.4 %collective-permute-start.3 = (bf16[1,1,32,2048]{3,2,1,0:T(8,128)(2,1)S(1)}, bf16[1,1,32,2048]{3,2,1,0:T(8,128)(2,1)}, u32[]{:S(2)}, u32[]{:S(2)}) collective-permute-start(bf16[1,1,32,2048]{3,2,1,0:T(8,128)(2,1)S(1)} %convert_element_type.57), channel_id=1, source_target_pairs={{1,0},{2,1},{3,2},{4,3},{5,4},{6,5},{7,6},{8,7},{9,8},{10,9},{11,1... | collective-permute-start | bytes 393224 | tf_op jit(solution)/shard_map/ppermute | solution.py:18
  84.7 3.5 copy-start.10
  84.7 3.5 copy-start.12
  90.8 14.6 %collective-permute-start.4 = (bf16[1,1,32,4096]{3,2,1,0:T(8,128)(2,1)S(1)}, bf16[1,1,32,4096]{3,2,1,0:T(8,128)(2,1)S(1)}, u32[]{:S(2)}, u32[]{:S(2)}) collective-permute-start(bf16[1,1,32,4096]{3,2,1,0:T(8,128)(2,1)S(1)} %reshape.106), channel_id=1, source_target_pairs={{0,1},{1,2},{2,3},{3,4},{4,5},{5,6},{6,7},{7,8},{8,9},{9,10},{10,1... | collective-permute-start | bytes 786440 | tf_op jit(solution)/shard_map/ppermute | solution.py:16
  95.7 9.8 %collective-permute-start.5 = (bf16[1,1,32,4096]{3,2,1,0:T(8,128)(2,1)S(1)}, bf16[1,1,32,4096]{3,2,1,0:T(8,128)(2,1)S(1)}, u32[]{:S(2)}, u32[]{:S(2)}) collective-permute-start(bf16[1,1,32,4096]{3,2,1,0:T(8,128)(2,1)S(1)} %reshape.106), channel_id=1, source_target_pairs={{1,0},{2,1},{3,2},{4,3},{5,4},{6,5},{7,6},{8,7},{9,8},{10,9},{11,1... | collective-permute-start | bytes 786440 | tf_op jit(solution)/shard_map/ppermute | solution.py:18
  106.5 3.8 slice-start
  106.6 3.7 slice-start.1
  111.1 1.4 copy-start.2
  118.8 160.1 %collective-permute-start.6 = (bf16[1,1,64,4096]{3,2,1,0:T(8,128)(2,1)}, bf16[1,1,64,4096]{3,2,1,0:T(8,128)(2,1)}, u32[]{:S(2)}, u32[]{:S(2)}) collective-permute-start(bf16[1,1,64,4096]{3,2,1,0:T(8,128)(2,1)} %get-tuple-element.45), channel_id=1, source_target_pairs={{0,1},{1,2},{2,3},{3,4},{4,5},{5,6},{6,7},{7,8},{8,9},{9,10},{10,1... | collective-permute-start | bytes 1572872 | tf_op jit(solution)/shard_map/ppermute | solution.py:16
  124.5 157.2 %collective-permute-start.7 = (bf16[1,1,64,4096]{3,2,1,0:T(8,128)(2,1)}, bf16[1,1,64,4096]{3,2,1,0:T(8,128)(2,1)}, u32[]{:S(2)}, u32[]{:S(2)}) collective-permute-start(bf16[1,1,64,4096]{3,2,1,0:T(8,128)(2,1)} %get-tuple-element.46), channel_id=1, source_target_pairs={{1,0},{2,1},{3,2},{4,3},{5,4},{6,5},{7,6},{8,7},{9,8},{10,9},{11,1... | collective-permute-start | bytes 1572872 | tf_op jit(solution)/shard_map/ppermute | solution.py:18
  125.7 69.1 %copy-start.6 = (f32[128]{0:T(128)S(1)}, f32[128]{0:T(128)}, u32[]{:S(2)}) copy-start(f32[128]{0:T(128)} %get-tuple-element.39) | copy-start | bytes 1540
  290.7 3.3 copy-start.8
  294.0 21.3 %copy-start.5 = (pred[8,9]{1,0:T(8,128)(4,1)S(1)}, pred[8,9]{1,0:T(8,128)(4,1)}, u32[]{:S(2)}) copy-start(pred[8,9]{1,0:T(8,128)(4,1)} %constant.34) | copy-start | bytes 220
  312.1 152.5 %copy-start.1 = (bf16[3,3,3,64,128]{4,3,2,1,0:T(8,128)(2,1)S(1)}, bf16[3,3,3,64,128]{4,3,2,1,0:T(8,128)(2,1)}, u32[]{:S(2)}) copy-start(bf16[3,3,3,64,128]{4,3,2,1,0:T(8,128)(2,1)} %param.9) | copy-start | bytes 1327108
Sparse Core Ops, SparseCore 0:
  194.9 265.5 all-reduce.3
where the time goes:
time: 481 us; the launch traced here: 472 us
  waiting for transfers between devices  157 us (33%)
  matrix products  108 us (22%)
  blocking collectives  83 us (17%)
  local copies, waits for them, and re-layouts  64.9 us (13%)
  starting transfers between devices  25 us (5%)
  other arithmetic  19.1 us (4%)
  between operations  15 us (3%)
    psum x1, waiting for transfers between devices, local(): gw_one, gb_one = lax.psum((gw_one, gb_one), ('dp', 'space'))  144 us
    psum x1, blocking collectives, local(): gw_one, gb_one = lax.psum((gw_one, gb_one), ('dp', 'space'))  83 us
    conv_general_dilated x2, matrix products, weight_grad(): lax.conv_general_dilated(padded, delta, (1, 1, 1), ((0, 0), (1, 1), (1, 1...  74.3 us
    conv_general_dilated x2, matrix products, input_grad(): lax.conv_general_dilated(delta, kernel[::-1, ::-1, ::-1], (1, 1, 1), (dep...  20.6 us
    ppermute x4, starting transfers between devices, padded_2(): lax.ppermute(tail, axis, [(i, (i + 1) % count) for i in range(ends)])  19.2 us
    reshape x2, local copies, waits for them, and re-layouts, local(): padded_2(act_in, (('space', 1),), 1)  15 us
    conv_general_dilated x2, matrix products, forward_conv(): lax.conv_general_dilated(padded, kernel, (1, 1, 1), ((0, 0), (1, 1), (1,...  12.8 us
    concatenate x8, local copies, waits for them, and re-layouts, padded_2(): jnp.concatenate([lax.ppermute(tail, axis, [(i, (i + 1) % count) for i in...  10.2 us
  transfers between devices with their start and end apart: 9, of which 3 were waited for; matrix products, arithmetic and copies ran while one was open for 29% of the time, Pallas kernels for 0%

commit v1 on v0

--- a/solution.py
+++ b/solution.py
@@ -103,7 +103,10 @@
         delta_one.reshape(samples, slab, side, side * chan_mid), (("space", 1),), 1
     ).reshape(samples, slab + 2, side, side, chan_mid)
     grad_x = input_grad(delta_one_pad, weight_one, (0, 0))
-    gw_one, gb_one = lax.psum((gw_one, gb_one), ("dp", "space"))
+    bars_wrap = lambda here_x, chip_axis, peer_axis: lax.psum(
+        lax.psum(here_x, axis_name=chip_axis), axis_name=peer_axis
+    )
+    gw_one, gb_one = bars_wrap((gw_one, gb_one), "dp", "space")
     grad_input = grad_x.astype(jnp.bfloat16).reshape(samples, slab, side, side * chan_in)
     return (
         grad_input,

time: 481 us -> 876 us (1.82)
  the two profiles are of different devices: /device:TPU:1 before, /device:TPU:8 now
where the time goes in v1:
time: 876 us; the launch traced here: 867 us
  waiting for transfers between devices  472 us (54%)
  blocking collectives  149 us (17%)
  matrix products  125 us (14%)
  local copies, waits for them, and re-layouts  63.9 us (7%)
  starting transfers between devices  24 us (3%)
  other arithmetic  18.7 us (2%)
  between operations  14.6 us (2%)
    psum x1, waiting for transfers between devices, local(): gw_two, gb_two = lax.psum((gw_two, gb_two), ('dp', 'space'))  267 us
    psum x1, waiting for transfers between devices, local(): lax.psum(lax.psum(here_x, axis_name=chip_axis), axis_name=peer_axis)  134 us
    conv_general_dilated x2, matrix products, weight_grad(): lax.conv_general_dilated(padded, delta, (1, 1, 1), ((0, 0), (1, 1), (1, 1...  91.8 us
    psum x1, blocking collectives, local(): gw_two, gb_two = lax.psum((gw_two, gb_two), ('dp', 'space'))  79.7 us
    psum x1, waiting for transfers between devices, local(): lax.psum(here_x, axis_name=chip_axis)  57 us
    psum x1, blocking collectives, local(): lax.psum(lax.psum(here_x, axis_name=chip_axis), axis_name=peer_axis)  36.3 us
    psum x1, blocking collectives, local(): lax.psum(here_x, axis_name=chip_axis)  32.6 us
    conv_general_dilated x2, matrix products, input_grad(): lax.conv_general_dilated(delta, kernel[::-1, ::-1, ::-1], (1, 1, 1), (dep...  20.5 us
  transfers between devices with their start and end apart: 11, of which 5 were waited for; matrix products, arithmetic and copies ran while one was open for 5% of the time, Pallas kernels for 0%

profile of v1, /device:TPU:8, one launch (start us, length us, event | category | flops | bytes accessed | tf_op | source)
XLA Modules:
  0.0 867.0 jit_solution(10501670810367410610)
XLA Ops:
  7.2 1.6 copy.175
  8.9 3.9 collective-permute-start
  12.7 1.3 collective-permute-start.1
  14.0 9.8 %collective-permute-done = bf16[1,1,64,2048]{2,3,1,0:T(8,128)(2,1)S(1)} collective-permute-done((bf16[1,1,64,2048]{2,3,1,0:T(8,128)(2,1)S(1)}, bf16[1,1,64,2048]{2,3,1,0:T(8,128)(2,1)S(1)}, u32[]{:S(2)}, u32[]{:S(2)}) %collective-permute-start) | collective-permute-done | bytes 262176 | tf_op jit(solution)/shard_map/ppermute | solution.py:16
  23.9 4.3 collective-permute-done.1
  28.2 1.7 pad_maximum_fusion
  29.9 1.9 pad
  31.8 6.8 copy.179
  38.6 1.5 slice.27
  40.2 11.3 %fusion.16 = (f32[2,64,8,9,64]{4,2,3,1,0:T(8,128)S(1)}, f32[2,64,8,9,64]{4,2,3,1,0:T(8,128)}) fusion(f32[64]{0:T(128)S(1)} %copy-done.8, pred[8,9]{0,1:T(8,128)(4,1)S(1)} %copy-done.11, bf16[3,3,3,32,64]{4,3,2,1,0:T(8,128)(2,1)S(1)} %copy-done.6, bf16[4,64,1,7,2,32]{5,3,4,1,0,2:T(8,128)(2,1)S(1)} %slice.27, bf16[4,64,1,8,9,32]{5,3,4,1,0,2:T(8,128)(2,1)} %copy.179), kind=kOutput, calls=%fused_computation.18 | convolution fusion | flops 1018822656 | bytes 6238536 | tf_op jit(solution)/shard_map/conv_general_dilated | solution.py:26
  51.5 0.9 copy.180
  52.4 2.0 slice_reduce_fusion
  54.4 3.3 reduce_sum.36
  57.9 0.3 convert_element_type.57
  58.1 4.5 collective-permute-start.2
  62.8 1.8 collective-permute-start.3
  64.5 5.4 copy.198
  69.9 13.0 %copy.205 = bf16[1,4,64,64,32]{4,0,3,2,1:T(2,128)(2,1)} copy(bf16[1,4,64,64,32]{2,4,3,1,0:T(8,128)(2,1)S(1)} %bitcast.106) | data formatting | bytes 2097152 | tf_op jit(solution)/shard_map/reshape | solution.py:74
  82.9 1.2 concatenate.41
  84.2 0.5 constant_dynamic-update-slice_fusion.1
  84.7 0.6 copy_dynamic-update-slice_fusion
  85.3 1.2 concatenate.42
  86.6 0.6 constant_dynamic-update-slice_fusion
  87.2 0.9 copy.236
  88.3 0.4 copy.188
  88.8 1.5 add_multiply_fusion.1
  90.5 0.3 convert_reduce_fusion.1
  90.9 5.0 collective-permute-start.4
  96.0 1.5 collective-permute-start.5
  97.5 8.1 fusion.56
  105.5 79.7 %psum.47 = f32[128]{0:T(128)} all-reduce(f32[128]{0:T(128)S(1)} %get-tuple-element.35), channel_id=1, replica_groups=mesh['dp'=16,'space'=16] {'dp','space'}, use_global_device_ids=true, to_apply=%region_9.10 | all-reduce | flops 128 | bytes 1024 | tf_op jit(solution)/shard_map/psum | solution.py:90
  185.4 0.3 copy.212
  185.8 0.4 copy.196
  186.3 2.5 fusion.47
  189.0 1.0 broadcast_in_dim.4
  190.1 0.8 fusion.17
  190.9 1.4 copy-done.2
  192.2 1.4 copy.238
  193.6 83.7 %fusion.18 = f32[3,3,3,32,64]{4,3,2,1,0:T(8,128)} fusion(bf16[1,4,64,64,32]{4,0,3,2,1:T(2,128)(2,1)S(1)} %bitcast.116, bf16[1,2,64,64,64]{4,3,2,1,0:T(8,128)(2,1)S(1)} %bitcast.108), kind=kOutput, calls=%fused_computation.25 | convolution fusion | flops 887193600 | bytes 2318336 | tf_op jit(solution)/shard_map/conv_general_dilated | solution.py:37
  277.4 0.5 broadcast_multiply_fusion.2
  278.2 2.5 reshape.107
  280.7 2.3 fusion.71
  282.9 4.8 collective-permute-start.6
  287.7 1.3 collective-permute-start.7
  288.9 2.8 convert_reduce_fusion
  291.8 32.6 %psum.44 = f32[64]{0:T(128)S(1)} all-reduce(f32[64]{0:T(128)S(1)} %convert_reduce_fusion), channel_id=1, replica_groups=mesh['dp'=16,'space'=16] {'dp'}, use_global_device_ids=true, to_apply=%region_5.0 | all-reduce | flops 64 | bytes 512 | tf_op jit(solution)/shard_map/psum | solution.py:107
  324.3 36.3 %psum.45 = f32[64]{0:T(128)S(1)} all-reduce(f32[64]{0:T(128)S(1)} %psum.44), channel_id=1, replica_groups=mesh['dp'=16,'space'=16] {'space'}, use_global_device_ids=true, to_apply=%region_6.0 | all-reduce | flops 64 | bytes 512 | tf_op jit(solution)/shard_map/psum | solution.py:106
  360.7 0.5 broadcast_multiply_fusion.3
  361.2 57.0 %all-reduce.4.cloned.1.call-done = f32[3,3,3,32,64]{4,3,2,1,0:T(8,128)} async-done(((f32[3,3,3,32,64]{4,3,2,1,0:T(8,128)}), f32[3,3,3,32,64]{4,3,2,1,0:T(8,128)}) %all-reduce.4.cloned.1.call-update) | async-done | bytes 221200 | tf_op jit(solution)/shard_map/psum | solution.py:107
  418.3 267.2 %all-reduce.8.cloned.1.call-done = f32[3,3,3,64,128]{4,3,2,1,0:T(8,128)} async-done(((f32[3,3,3,64,128]{4,3,2,1,0:T(8,128)}), f32[3,3,3,64,128]{4,3,2,1,0:T(8,128)}) %all-reduce.8.cloned.1.call-update) | async-done | bytes 884752 | tf_op jit(solution)/shard_map/psum | solution.py:90
  685.4 2.2 broadcast_multiply_fusion
  687.6 133.6 %all-reduce.6.cloned.1.call-done = f32[3,3,3,32,64]{4,3,2,1,0:T(8,128)} async-done(((f32[3,3,3,32,64]{4,3,2,1,0:T(8,128)}), f32[3,3,3,32,64]{4,3,2,1,0:T(8,128)}) %all-reduce.6.cloned.1.call-update) | async-done | bytes 221200 | tf_op jit(solution)/shard_map/psum | solution.py:106
  821.2 1.8 broadcast_multiply_fusion.1
  823.0 2.8 concatenate.34
  825.8 2.1 concatenate.35
  827.9 2.2 maximum_bitcast_fusion
  830.1 2.7 copy.213
  832.9 1.3 pad.6.clone
  834.1 3.0 copy.203
  837.2 0.3 slice.36
  837.5 18.0 %fusion.4 = bf16[2,64,8,9,32]{4,2,3,1,0:T(8,128)(2,1)} fusion(bf16[3,3,3,32,64]{4,3,2,1,0:T(8,128)(2,1)S(1)} %copy-done.7, bf16[4,64,1,7,2,64]{5,3,4,1,0,2:T(8,128)(2,1)S(1)} %slice.36, bf16[4,64,1,8,9,64]{5,3,4,1,0,2:T(8,128)(2,1)S(1)} %copy.203), kind=kOutput, calls=%fused_computation.6 | convolution fusion | flops 1017249792 | bytes 3518464 | tf_op jit(solution)/shard_map/conv_general_dilated | solution.py:48
  855.6 3.2 copy.204
  858.7 0.3 select_convert_fusion
  859.1 1.1 copy.208
  (65 shorter events, 1.9 us)
Async XLA Ops:
  7.2 81.6 %copy-start = (bf16[3,3,3,64,128]{4,3,2,1,0:T(8,128)(2,1)S(1)}, bf16[3,3,3,64,128]{4,3,2,1,0:T(8,128)(2,1)}, u32[]{:S(2)}) copy-start(bf16[3,3,3,64,128]{4,3,2,1,0:T(8,128)(2,1)} %param.9) | copy-start | bytes 1327108
  7.2 411.1 %all-reduce.4.cloned.1.call-start = ((), (), s32[]{:S(2)}) async-start(), calls=%async_computation | async-start | bytes 884736 | tf_op jit(solution)/shard_map/psum | solution.py:107
  8.8 15.1 %copy-start.3 = (bf16[1,2,64,2048]{2,3,1,0:T(8,128)(2,1)}, bf16[1,2,64,2048]{2,3,1,0:T(8,128)(2,1)S(1)}, u32[]{:S(2)}) copy-start(bf16[1,2,64,2048]{2,3,1,0:T(8,128)(2,1)S(1)} %copy.175) | copy-start | bytes 1572868
  8.9 15.0 %collective-permute-start = (bf16[1,1,64,2048]{2,3,1,0:T(8,128)(2,1)S(1)}, bf16[1,1,64,2048]{2,3,1,0:T(8,128)(2,1)S(1)}, u32[]{:S(2)}, u32[]{:S(2)}) collective-permute-start(bf16[1,1,64,2048]{2,3,1,0:T(8,128)(2,1)S(1)} %get-tuple-element.43), channel_id=1, source_target_pairs={{0,1},{1,2},{2,3},{3,4},{4,5},{5,6},{6,7},{7,8},{8,9},{9,10},{10,1... | collective-permute-start | bytes 786440 | tf_op jit(solution)/shard_map/ppermute | solution.py:16
  12.7 15.4 %collective-permute-start.1 = (bf16[1,1,64,2048]{2,3,1,0:T(8,128)(2,1)S(1)}, bf16[1,1,64,2048]{2,3,1,0:T(8,128)(2,1)S(1)}, u32[]{:S(2)}, u32[]{:S(2)}) collective-permute-start(bf16[1,1,64,2048]{2,3,1,0:T(8,128)(2,1)S(1)} %get-tuple-element.44), channel_id=1, source_target_pairs={{1,0},{2,1},{3,2},{4,3},{5,4},{6,5},{7,6},{8,7},{9,8},{10,9},{11,1... | collective-permute-start | bytes 786440 | tf_op jit(solution)/shard_map/ppermute | solution.py:18
  31.8 8.3 copy-start.6
  31.8 8.3 copy-start.8
  31.8 8.3 copy-start.11
  52.4 10.3 %copy-start.4 = (bf16[1,1,32,4096]{3,2,1,0:T(8,128)(2,1)S(1)}, bf16[1,1,32,4096]{3,2,1,0:T(8,128)(2,1)}, u32[]{:S(2)}) copy-start(bf16[1,1,32,4096]{3,2,1,0:T(8,128)(2,1)} %param.11) | copy-start | bytes 786436
  58.1 24.8 %collective-permute-start.2 = (bf16[1,1,32,2048]{3,2,1,0:T(8,128)(2,1)S(1)}, bf16[1,1,32,2048]{3,2,1,0:T(8,128)(2,1)}, u32[]{:S(2)}, u32[]{:S(2)}) collective-permute-start(bf16[1,1,32,2048]{3,2,1,0:T(8,128)(2,1)S(1)} %convert_element_type.57), channel_id=1, source_target_pairs={{0,1},{1,2},{2,3},{3,4},{4,5},{5,6},{6,7},{7,8},{8,9},{9,10},{10,1... | collective-permute-start | bytes 393224 | tf_op jit(solution)/shard_map/ppermute | solution.py:16
  62.8 22.6 %collective-permute-start.3 = (bf16[1,1,32,2048]{3,2,1,0:T(8,128)(2,1)S(1)}, bf16[1,1,32,2048]{3,2,1,0:T(8,128)(2,1)}, u32[]{:S(2)}, u32[]{:S(2)}) collective-permute-start(bf16[1,1,32,2048]{3,2,1,0:T(8,128)(2,1)S(1)} %convert_element_type.57), channel_id=1, source_target_pairs={{1,0},{2,1},{3,2},{4,3},{5,4},{6,5},{7,6},{8,7},{9,8},{10,9},{11,1... | collective-permute-start | bytes 393224 | tf_op jit(solution)/shard_map/ppermute | solution.py:18
  85.3 3.5 copy-start.9
  85.3 3.5 copy-start.12
  90.9 94.3 %collective-permute-start.4 = (bf16[1,1,32,4096]{3,2,1,0:T(8,128)(2,1)S(1)}, bf16[1,1,32,4096]{3,2,1,0:T(8,128)(2,1)S(1)}, u32[]{:S(2)}, u32[]{:S(2)}) collective-permute-start(bf16[1,1,32,4096]{3,2,1,0:T(8,128)(2,1)S(1)} %reshape.106), channel_id=1, source_target_pairs={{0,1},{1,2},{2,3},{3,4},{4,5},{5,6},{6,7},{7,8},{8,9},{9,10},{10,1... | collective-permute-start | bytes 786440 | tf_op jit(solution)/shard_map/ppermute | solution.py:16
  96.0 89.3 %collective-permute-start.5 = (bf16[1,1,32,4096]{3,2,1,0:T(8,128)(2,1)S(1)}, bf16[1,1,32,4096]{3,2,1,0:T(8,128)(2,1)S(1)}, u32[]{:S(2)}, u32[]{:S(2)}) collective-permute-start(bf16[1,1,32,4096]{3,2,1,0:T(8,128)(2,1)S(1)} %reshape.106), channel_id=1, source_target_pairs={{1,0},{2,1},{3,2},{4,3},{5,4},{6,5},{7,6},{8,7},{9,8},{10,9},{11,1... | collective-permute-start | bytes 786440 | tf_op jit(solution)/shard_map/ppermute | solution.py:18
  186.2 3.8 slice-start
  186.3 3.7 slice-start.1
  188.8 4.8 slice-start.2
  190.1 3.6 slice-start.3
  190.9 1.4 copy-start.2
  193.6 83.8 %copy-start.10 = (f32[128]{0:T(128)S(1)}, f32[128]{0:T(128)}, u32[]{:S(2)}) copy-start(f32[128]{0:T(128)} %psum.47) | copy-start | bytes 1540
  277.4 408.0 %all-reduce.8.cloned.1.call-start = ((), (), s32[]{:S(2)}) async-start(), calls=%async_computation.2 | async-start | bytes 1769472 | tf_op jit(solution)/shard_map/psum | solution.py:90
  278.1 543.1 %all-reduce.6.cloned.1.call-start = ((), (), s32[]{:S(2)}) async-start(), calls=%async_computation.1 | async-start | bytes 884736 | tf_op jit(solution)/shard_map/psum | solution.py:106
  282.9 540.1 %collective-permute-start.6 = (bf16[1,1,64,4096]{3,2,1,0:T(8,128)(2,1)}, bf16[1,1,64,4096]{3,2,1,0:T(8,128)(2,1)}, u32[]{:S(2)}, u32[]{:S(2)}) collective-permute-start(bf16[1,1,64,4096]{3,2,1,0:T(8,128)(2,1)} %get-tuple-element.41), channel_id=1, source_target_pairs={{0,1},{1,2},{2,3},{3,4},{4,5},{5,6},{6,7},{7,8},{8,9},{9,10},{10,1... | collective-permute-start | bytes 1572872 | tf_op jit(solution)/shard_map/ppermute | solution.py:16
  287.7 538.2 %collective-permute-start.7 = (bf16[1,1,64,4096]{3,2,1,0:T(8,128)(2,1)}, bf16[1,1,64,4096]{3,2,1,0:T(8,128)(2,1)S(1)}, u32[]{:S(2)}, u32[]{:S(2)}) collective-permute-start(bf16[1,1,64,4096]{3,2,1,0:T(8,128)(2,1)} %get-tuple-element.42), channel_id=1, source_target_pairs={{1,0},{2,1},{3,2},{4,3},{5,4},{6,5},{7,6},{8,7},{9,8},{10,9},{11,1... | collective-permute-start | bytes 1572872 | tf_op jit(solution)/shard_map/ppermute | solution.py:18
  834.1 3.3 copy-start.7
  837.5 21.2 %copy-start.5 = (pred[8,9]{1,0:T(8,128)(4,1)S(1)}, pred[8,9]{1,0:T(8,128)(4,1)}, u32[]{:S(2)}) copy-start(pred[8,9]{1,0:T(8,128)(4,1)} %constant.34) | copy-start | bytes 220
  837.5 22.8 %copy-start.1 = (bf16[3,3,3,64,128]{4,3,2,1,0:T(8,128)(2,1)S(1)}, bf16[3,3,3,64,128]{4,3,2,1,0:T(8,128)(2,1)}, u32[]{:S(2)}) copy-start(bf16[3,3,3,64,128]{4,3,2,1,0:T(8,128)(2,1)} %param.9) | copy-start | bytes 1327108
Sparse Core Ops, SparseCore 0:
  277.5 140.6 all-reduce.3
  424.3 261.0 all-reduce.7
  688.0 133.1 all-reduce.5
